TPU v7x, 32 devices: a whole 2x2x4 slice. The times are simulated.
32 devices in a mesh: frag: 2 (over x), occ: 2 (over core), vir: 8 (over z, y).
Axes of the slice: x: 2, y: 2, z: 4, core: 2. Of those that a mesh axis runs over, the one named last changes fastest.
Arguments:
- factors: bfloat16 [8, 1024, 3072], P(('frag', 'occ'), 'vir'), parts along dimension 0, may hold values from -2 to 2
- occ_energy: int32 [8], P('frag'), parts along dimension 0, may hold values from -1536 to -512
- vir_energy: int32 [2048], P('frag'), parts along dimension 0, may hold values from 512 to 4096
Outputs:
- density: float32 [8, 1024, 3072], P(('frag', 'occ'), 'vir'), parts along dimension 0
There are 2 independent parts, one for each index of `frag`. A program takes and returns all parts, laid end to end along the dimension named above; each array names one. Nothing has to cross between parts.
Inputs may be any that keep to these rules, and one draw needn't show every extreme that they name: `occ_energy`: occupied energies lie at or below the highest occupied level -512. `vir_energy`: virtual energies lie at or above the lowest virtual level 512.
All inputs are finite; a program needn't handle non-finite values.
Results may differ from a plain program's by a relative error of at most 0.0055.
Values may be sent and summed in bfloat16 or wider, within the bound.
No kernel may reach another device: no remote copies, remote signals or barrier semaphores. Data moves between devices by JAX's collectives and lax.ppermute only.
A program may use at most 128 MiB of HBM per device.

v0:
```python
import jax
import jax.numpy as jnp
from jax import lax
from jax.sharding import PartitionSpec as P

energy_unit = 1.0 / 1024.0


def on_device(factors, occ_energy, vir_energy):
    occ_local, vir_local, aux_count = factors.shape
    occ_count = lax.axis_size("occ")
    occ_start = lax.axis_index("occ") * occ_local
    vir_start = lax.axis_index("vir") * vir_local
    own_energy = lax.dynamic_slice_in_dim(occ_energy, occ_start, occ_local)
    vir_slice = lax.dynamic_slice_in_dim(vir_energy, vir_start, vir_local)
    base_sum = own_energy[:, None, None] - vir_slice[None, :, None] - vir_energy[None, None, :]
    gathered = None
    gathered = lax.all_gather(factors, "vir", axis=1, tiled=True)
    all_rows = lax.all_gather(gathered, "occ", axis=0, tiled=True)

    def loop_step(j, density):
        partner = lax.dynamic_index_in_dim(all_rows, j, 0, keepdims=False)
        direct = jnp.einsum(
            "iap,bp->iab", factors, partner, preferred_element_type=jnp.float32
        ).astype(jnp.bfloat16)
        swapped = lax.all_to_all(direct, "vir", split_axis=2, concat_axis=1, tiled=True)
        crossed = jnp.swapaxes(swapped, 1, 2)
        divisor = (base_sum + occ_energy[j]).astype(jnp.float32) * energy_unit
        amplitude = (
            (2.0 * direct.astype(jnp.float32) - crossed.astype(jnp.float32)) / divisor
        ).astype(jnp.bfloat16)
        return density + jnp.einsum(
            "iab,bp->iap", amplitude, partner, preferred_element_type=jnp.float32
        )

    start_density = jnp.zeros((occ_local, vir_local, aux_count), jnp.float32)
    return lax.fori_loop(0, occ_count * occ_local, loop_step, start_density)


def solution(mesh):
    return jax.shard_map(
        on_device,
        mesh=mesh,
        in_specs=(P(("frag", "occ"), "vir", None), P("frag"), P("frag")),
        out_specs=P(("frag", "occ"), "vir", None),
        check_vma=False,
    )
```

profile of v0, /device:TPU:0, one launch (start us, length us, event | category | flops | bytes accessed | tf_op | source)
XLA Modules:
  0.0 370.8 jit_solution(10798730904287225482)
XLA Ops:
  6.5 0.0 all-gather.3.cloned.1.call-start
  6.5 0.7 all-gather.3.cloned.1.call-update
  7.3 0.0 all-gather.5.cloned.1.call-start
  7.3 181.1 %all-gather.3.cloned.1.call-done = bf16[2,1024,3072]{2,1,0:T(8,128)(2,1)} async-done(((bf16[2,128,3072]{2,1,0:T(8,128)(2,1)}), bf16[2,1024,3072]{2,1,0:T(8,128)(2,1)}) %all-gather.3.cloned.1.call-update) | async-done | bytes 12582928 | tf_op jit(solution)/shard_map/all_gather | solution.py:18
  188.4 0.0 copy-start.1
  188.4 0.0 copy-start
  188.4 0.0 all-gather.5.cloned.1.call-update
  188.4 0.6 copy-done.1
  189.0 0.1 dynamic_slice.21
  189.1 0.0 copy-done
  189.1 0.1 dynamic_slice.22
  189.2 0.1 broadcast_subtract_fusion
  189.3 39.2 %all-gather.5.cloned.1.call-done = bf16[4,1024,3072]{2,1,0:T(8,128)(2,1)} async-done(((bf16[2,1024,3072]{2,1,0:T(8,128)(2,1)}), bf16[4,1024,3072]{2,1,0:T(8,128)(2,1)}) %all-gather.5.cloned.1.call-update) | async-done | bytes 25165840 | tf_op jit(solution)/shard_map/all_gather | solution.py:19
  228.4 135.5 %while.14 = (s32[]{:T(128)}, f32[2,128,3072]{2,1,0:T(8,128)}, bf16[4,1024,3072]{2,1,0:T(8,128)(2,1)}, bf16[2,128,3072]{2,1,0:T(8,128)(2,1)}, s32[4]{0:T(128)S(1)...) while((s32[]{:T(128)}, f32[2,128,3072]{2,1,0:T(8,128)}, ...), condition=%wide.region_1.2_spmd.clone, body=%wide.region_0.1_spmd.clone.sunk | while | flops 3225419776 | bytes 27792552 | solution.py:37
  228.4 5.1 %fusion.36 = bf16[2,128,1024]{1,2,0:T(8,128)(2,1)S(1)} fusion(bf16[2,128,3072]{2,1,0:T(8,128)(2,1)} %get-tuple-element.221, bf16[4,1024,3072]{2,1,0:T(8,128)(2,1)} %get-tuple-element.220, s32[]{:T(128)S(6)} %copy.16), kind=kOutput, calls=%fused_computation.9.clone.1 | convolution fusion | flops 1610874880 | bytes 8388612 | tf_op jit(solution)/shard_map/while/body/eval_jaxpr/iap,bp->iab/dot_general | solution.py:23
  233.5 1.4 copy.12
  234.9 5.8 %all-to-all-start = ((bf16[2,128,1024]{1,0,2:T(2,128)(2,1)}), bf16[2,128,1024]{1,0,2:T(2,128)(2,1)S(1)}, u32[]{:S(2)}, u32[]{:S(2)}) async-start(bf16[2,128,1024]{1,0,2:T(2,128)(2,1)} %copy.12), calls=%async_computation | async-start | bytes 1048576 | tf_op jit(solution)/shard_map/while/body/eval_jaxpr/all_to_all | solution.py:26
  240.6 0.7 dynamic_slice.44
  241.3 14.3 %all-to-all-done = bf16[2,128,1024]{1,0,2:T(2,128)(2,1)S(1)} async-done(((bf16[2,128,1024]{1,0,2:T(2,128)(2,1)}), bf16[2,128,1024]{1,0,2:T(2,128)(2,1)S(1)}, u32[]{:S(2)}, u32[]{:S(2)}) %all-to-all-start) | async-done | bytes 524320 | tf_op jit(solution)/shard_map/while/body/eval_jaxpr/all_to_all | solution.py:26
  255.6 0.4 copy.13
  256.0 1.1 fusion.37
  257.1 6.3 %fusion.38 = f32[2,128,3072]{2,1,0:T(8,128)} fusion(bf16[2,128,1024]{1,2,0:T(8,128)(2,1)S(1)} %fusion.37, bf16[4,1024,3072]{2,1,0:T(8,128)(2,1)} %get-tuple-element.220, s32[]{:T(128)S(6)} %copy.16, f32[2,128,3072]{2,1,0:T(8,128)} %get-tuple-element.210, pred[]{:T(512)S(6)} %compare.3), kind=kOutput, calls=%fused_computation.7.clone.1 | convolution fusion | flops 1612185600 | bytes 13107205 | tf_op jit(solution)/shard_map/while/body/eval_jaxpr/iab,bp->iap/dot_general | solution.py:32
  263.4 5.0 %fusion.36 = bf16[2,128,1024]{1,2,0:T(8,128)(2,1)S(1)} fusion(bf16[2,128,3072]{2,1,0:T(8,128)(2,1)} %get-tuple-element.221, bf16[4,1024,3072]{2,1,0:T(8,128)(2,1)} %get-tuple-element.220, s32[]{:T(128)S(6)} %copy.16), kind=kOutput, calls=%fused_computation.9.clone.1 | convolution fusion | flops 1610874880 | bytes 8388612 | tf_op jit(solution)/shard_map/while/body/eval_jaxpr/iap,bp->iab/dot_general | solution.py:23
  268.5 1.4 copy.12
  269.8 3.6 all-to-all-start
  273.5 0.7 dynamic_slice.44
  274.1 14.0 %all-to-all-done = bf16[2,128,1024]{1,0,2:T(2,128)(2,1)S(1)} async-done(((bf16[2,128,1024]{1,0,2:T(2,128)(2,1)}), bf16[2,128,1024]{1,0,2:T(2,128)(2,1)S(1)}, u32[]{:S(2)}, u32[]{:S(2)}) %all-to-all-start) | async-done | bytes 524320 | tf_op jit(solution)/shard_map/while/body/eval_jaxpr/all_to_all | solution.py:26
  288.2 0.4 copy.13
  288.6 1.1 fusion.37
  289.7 7.3 %fusion.38 = f32[2,128,3072]{2,1,0:T(8,128)} fusion(bf16[2,128,1024]{1,2,0:T(8,128)(2,1)S(1)} %fusion.37, bf16[4,1024,3072]{2,1,0:T(8,128)(2,1)} %get-tuple-element.220, s32[]{:T(128)S(6)} %copy.16, f32[2,128,3072]{2,1,0:T(8,128)} %get-tuple-element.210, pred[]{:T(512)S(6)} %compare.3), kind=kOutput, calls=%fused_computation.7.clone.1 | convolution fusion | flops 1612185600 | bytes 13107205 | tf_op jit(solution)/shard_map/while/body/eval_jaxpr/iab,bp->iap/dot_general | solution.py:32
  296.9 5.0 %fusion.36 = bf16[2,128,1024]{1,2,0:T(8,128)(2,1)S(1)} fusion(bf16[2,128,3072]{2,1,0:T(8,128)(2,1)} %get-tuple-element.221, bf16[4,1024,3072]{2,1,0:T(8,128)(2,1)} %get-tuple-element.220, s32[]{:T(128)S(6)} %copy.16), kind=kOutput, calls=%fused_computation.9.clone.1 | convolution fusion | flops 1610874880 | bytes 8388612 | tf_op jit(solution)/shard_map/while/body/eval_jaxpr/iap,bp->iab/dot_general | solution.py:23
  302.0 1.4 copy.12
  303.3 3.6 all-to-all-start
  307.0 0.7 dynamic_slice.44
  307.6 14.0 %all-to-all-done = bf16[2,128,1024]{1,0,2:T(2,128)(2,1)S(1)} async-done(((bf16[2,128,1024]{1,0,2:T(2,128)(2,1)}), bf16[2,128,1024]{1,0,2:T(2,128)(2,1)S(1)}, u32[]{:S(2)}, u32[]{:S(2)}) %all-to-all-start) | async-done | bytes 524320 | tf_op jit(solution)/shard_map/while/body/eval_jaxpr/all_to_all | solution.py:26
  321.7 0.4 copy.13
  322.1 1.1 fusion.37
  323.2 7.3 %fusion.38 = f32[2,128,3072]{2,1,0:T(8,128)} fusion(bf16[2,128,1024]{1,2,0:T(8,128)(2,1)S(1)} %fusion.37, bf16[4,1024,3072]{2,1,0:T(8,128)(2,1)} %get-tuple-element.220, s32[]{:T(128)S(6)} %copy.16, f32[2,128,3072]{2,1,0:T(8,128)} %get-tuple-element.210, pred[]{:T(512)S(6)} %compare.3), kind=kOutput, calls=%fused_computation.7.clone.1 | convolution fusion | flops 1612185600 | bytes 13107205 | tf_op jit(solution)/shard_map/while/body/eval_jaxpr/iab,bp->iap/dot_general | solution.py:32
  330.4 5.0 %fusion.36 = bf16[2,128,1024]{1,2,0:T(8,128)(2,1)S(1)} fusion(bf16[2,128,3072]{2,1,0:T(8,128)(2,1)} %get-tuple-element.221, bf16[4,1024,3072]{2,1,0:T(8,128)(2,1)} %get-tuple-element.220, s32[]{:T(128)S(6)} %copy.16), kind=kOutput, calls=%fused_computation.9.clone.1 | convolution fusion | flops 1610874880 | bytes 8388612 | tf_op jit(solution)/shard_map/while/body/eval_jaxpr/iap,bp->iab/dot_general | solution.py:23
  335.5 1.4 copy.12
  336.8 3.6 all-to-all-start
  340.5 0.7 dynamic_slice.44
  341.1 14.0 %all-to-all-done = bf16[2,128,1024]{1,0,2:T(2,128)(2,1)S(1)} async-done(((bf16[2,128,1024]{1,0,2:T(2,128)(2,1)}), bf16[2,128,1024]{1,0,2:T(2,128)(2,1)S(1)}, u32[]{:S(2)}, u32[]{:S(2)}) %all-to-all-start) | async-done | bytes 524320 | tf_op jit(solution)/shard_map/while/body/eval_jaxpr/all_to_all | solution.py:26
  355.2 0.4 copy.13
  355.6 1.1 fusion.37
  356.7 7.3 %fusion.38 = f32[2,128,3072]{2,1,0:T(8,128)} fusion(bf16[2,128,1024]{1,2,0:T(8,128)(2,1)S(1)} %fusion.37, bf16[4,1024,3072]{2,1,0:T(8,128)(2,1)} %get-tuple-element.220, s32[]{:T(128)S(6)} %copy.16, f32[2,128,3072]{2,1,0:T(8,128)} %get-tuple-element.210, pred[]{:T(512)S(6)} %compare.3), kind=kOutput, calls=%fused_computation.7.clone.1 | convolution fusion | flops 1612185600 | bytes 13107205 | tf_op jit(solution)/shard_map/while/body/eval_jaxpr/iab,bp->iap/dot_general | solution.py:32
  (1 shorter events, 0.0 us)
Async XLA Ops:
  6.5 181.8 %all-gather.3.cloned.1.call-start = ((), (), s32[]{:S(2)}) async-start(), calls=%async_computation.1 | async-start | bytes 14155776 | tf_op jit(solution)/shard_map/all_gather | solution.py:18
  7.3 221.2 %all-gather.5.cloned.1.call-start = ((), (), s32[]{:S(2)}) async-start(), calls=%async_computation.2 | async-start | bytes 37748736 | tf_op jit(solution)/shard_map/all_gather | solution.py:19
  188.4 0.7 copy-start.1
  188.4 0.7 copy-start
  234.9 20.7 %all-to-all-start = ((bf16[2,128,1024]{1,0,2:T(2,128)(2,1)}), bf16[2,128,1024]{1,0,2:T(2,128)(2,1)S(1)}, u32[]{:S(2)}, u32[]{:S(2)}) async-start(bf16[2,128,1024]{1,0,2:T(2,128)(2,1)} %copy.12), calls=%async_computation | async-start | bytes 1048576 | tf_op jit(solution)/shard_map/while/body/eval_jaxpr/all_to_all | solution.py:26
  269.8 18.3 %all-to-all-start = ((bf16[2,128,1024]{1,0,2:T(2,128)(2,1)}), bf16[2,128,1024]{1,0,2:T(2,128)(2,1)S(1)}, u32[]{:S(2)}, u32[]{:S(2)}) async-start(bf16[2,128,1024]{1,0,2:T(2,128)(2,1)} %copy.12), calls=%async_computation | async-start | bytes 1048576 | tf_op jit(solution)/shard_map/while/body/eval_jaxpr/all_to_all | solution.py:26
  303.3 18.3 %all-to-all-start = ((bf16[2,128,1024]{1,0,2:T(2,128)(2,1)}), bf16[2,128,1024]{1,0,2:T(2,128)(2,1)S(1)}, u32[]{:S(2)}, u32[]{:S(2)}) async-start(bf16[2,128,1024]{1,0,2:T(2,128)(2,1)} %copy.12), calls=%async_computation | async-start | bytes 1048576 | tf_op jit(solution)/shard_map/while/body/eval_jaxpr/all_to_all | solution.py:26
  336.8 18.3 %all-to-all-start = ((bf16[2,128,1024]{1,0,2:T(2,128)(2,1)}), bf16[2,128,1024]{1,0,2:T(2,128)(2,1)S(1)}, u32[]{:S(2)}, u32[]{:S(2)}) async-start(bf16[2,128,1024]{1,0,2:T(2,128)(2,1)} %copy.12), calls=%async_computation | async-start | bytes 1048576 | tf_op jit(solution)/shard_map/while/body/eval_jaxpr/all_to_all | solution.py:26
Sparse Core Ops, SparseCore 0:
  9.5 178.8 all-gather.2
  189.9 38.4 all-gather.4
where the time goes:
time: 371 us
  waiting for transfers between devices  277 us (75%)
  matrix products  48.3 us (13%)
  starting transfers between devices  16.7 us (5%)
  between operations  13.4 us (4%)
  local copies, waits for them, and re-layouts  10.5 us (3%)
  other arithmetic  4.39 us (1%)
    all_gather x1, waiting for transfers between devices, on_device(): gathered = lax.all_gather(factors, 'vir', axis=1, tiled=True)  181 us
    all_to_all x4, waiting for transfers between devices, loop_step(): lax.all_to_all(direct, 'vir', split_axis=2, concat_axis=1, tiled=True)  56.3 us
    all_gather x1, waiting for transfers between devices, on_device(): all_rows = lax.all_gather(gathered, 'occ', axis=0, tiled=True)  39.2 us
    dot_general x4, matrix products, loop_step(): jnp.einsum('iab,bp->iap', amplitude, partner, preferred_element_type=jnp....  28.2 us
    dot_general x4, matrix products, loop_step(): jnp.einsum('iap,bp->iab', factors, partner, preferred_element_type=jnp.fl...  20.2 us
    all_to_all x4, starting transfers between devices, loop_step(): lax.all_to_all(direct, 'vir', split_axis=2, concat_axis=1, tiled=True)  16.7 us
  transfers between devices with their start and end apart: 6, of which 6 were waited for; matrix products, arithmetic and copies ran while one was open for 1% of the time, Pallas kernels for 0%

commit v1 on v0

v1 whole, which is shorter than its diff:
```python
import functools

import jax
import jax.numpy as jnp
import numpy as np
from jax import lax
from jax.experimental import pallas as pl
from jax.experimental.pallas import tpu as pltpu
from jax.sharding import PartitionSpec as P

energy_unit = 1.0 / 1024.0


last_cuts = 1

across = (((1,), (1,)), ((), ()))
along = (((1,), (0,)), ((), ()))


def ring_order(mesh, axis):
    devices = mesh.devices
    for name in reversed(mesh.axis_names):
        if name != axis:
            devices = devices[(slice(None),) * mesh.axis_names.index(name) + (0,)]
    count = len(devices)
    spots = [tuple(getattr(device, "coords", ())) for device in devices]
    widths = [len(set(values)) for values in zip(*spots)] if all(spots) else []
    if sorted(widths)[-2:-1] == [2] and sorted(widths)[-1] * 2 == count:
        long = max(range(len(widths)), key=lambda d: widths[d])
        short = [d for d in range(len(widths)) if widths[d] == 2 and d != long][0]
        low = min(spot[short] for spot in spots)
        there = sorted((k for k in range(count) if spots[k][short] == low), key=lambda k: spots[k][long])
        back = sorted((k for k in range(count) if spots[k][short] != low), key=lambda k: -spots[k][long])
        return there + back
    return list(range(count))


def cut_kernel(source, *refs):
    *pieces, sems = refs
    rows = pieces[0].shape[1]
    copies = [
        pltpu.make_async_copy(source.at[:, pl.ds(k * rows, rows), :], piece, sems.at[k])
        for k, piece in enumerate(pieces)
    ]
    for copy in copies:
        copy.start()
    for copy in copies:
        copy.wait()


def cut(source, count):
    local, rows, aux = source.shape
    vmem = pl.BlockSpec(memory_space=pltpu.VMEM)
    return pl.pallas_call(
        cut_kernel,
        out_shape=[jax.ShapeDtypeStruct((local, rows // count, aux), source.dtype)] * count,
        in_specs=[pl.BlockSpec(memory_space=pltpu.HBM)],
        out_specs=[vmem] * count,
        scratch_shapes=[pltpu.SemaphoreType.DMA((count,))],
        compiler_params=pltpu.CompilerParams(vmem_limit_bytes=8 * 1024 * 1024),
        name="cut",
    )(source)


def block_kernel(layout, occ_pairs, own_vir, vir_rows, *refs):
    number, parts, count, steps, tiles, prior, stage = layout
    refs = list(refs)
    own = [refs.pop(0) for _ in range(1 if stage == 2 else parts)]
    if number:
        groups = [[refs.pop(0) for _ in range(count)] for _ in range(1 if stage == 1 else parts)]
    else:
        groups = [[block] for block in own]
    near_amplitude, near_swapped = (refs.pop(0), refs.pop(0)) if stage == 2 else (None, None)
    density_in = refs.pop(0) if prior and stage != 1 else None
    near_out, swapped_out = (refs.pop(0), refs.pop(0)) if stage == 1 else (None, None)
    density_out = refs.pop(0) if stage != 1 else None
    direct = refs.pop(0)
    amplitude, density, out_sem, in_sem = refs if stage != 1 else (near_out, None, None, None)
    local, rows, aux = own[0].shape
    step, depth = aux // tiles, aux // steps
    total = parts * local
    wide = local * rows
    width = sum(piece.shape[1] for piece in groups[0])
    span = local * width
    fresh = [part for part in range(len(groups)) if part or stage != 2]
    starts = {part: (0 if part == 0 else ((parts if stage != 2 else 0) + part - 1) * wide) for part in fresh}

    def tile_copy(start, inward):
        columns = pl.ds(start * step, step)
        if inward:
            return pltpu.make_async_copy(density_in.at[:, :, columns], density.at[:, :, columns], in_sem.at[start])
        return pltpu.make_async_copy(density.at[:, :, columns], density_out.at[:, :, columns], out_sem.at[start])

    if density_in is not None:
        for start in range(tiles):
            tile_copy(start, True).start()

    def stack(arrays):
        return jnp.concatenate(arrays, axis=0) if len(arrays) > 1 else arrays[0]

    def lines(group, columns):
        return [piece[k, :, columns] for k in range(local) for piece in group]

    def depth_step(k, carry):
        columns = pl.ds(pl.multiple_of(k * depth, depth), depth)
        all_rows = stack([block[:, :, columns].reshape(wide, depth) for block in own])
        for part in fresh:
            left = all_rows if part == 0 else all_rows[:wide]
            right = stack(lines(groups[part], columns))
            term = lax.dot_general(left, right, across, preferred_element_type=jnp.float32)
            at = pl.ds(starts[part], left.shape[0])
            direct[at, :] = direct[at, :] + term
        return carry

    direct[...] = jnp.zeros_like(direct)
    lax.fori_loop(0, steps, depth_step, 0)
    vir_pair = own_vir[...] + vir_rows[number][:, :width]

    def tile(row, column, array=direct):
        sums = array[row * rows : (row + 1) * rows, column * width : (column + 1) * width]
        return sums.astype(jnp.bfloat16).astype(jnp.float32)

    for i in range(local):
        for part in fresh:
            for k in range(local):
                j = part * local + k
                divisor = (occ_pairs[i * total + j][:, :width] - vir_pair).astype(jnp.float32) * energy_unit
                straight = tile(starts[part] // rows + i, k)
                crossed = tile(j - local, i, near_swapped) if stage == 2 else tile(j, i)
                here = slice(j * width, (j + 1) * width)
                top = 2.0 * straight - crossed
                amplitude[i * rows : (i + 1) * rows, here] = (top / divisor).astype(jnp.bfloat16)
    if stage == 1:
        swapped_out[...] = direct[wide:, :].astype(jnp.bfloat16)
        return
    if stage == 2:
        amplitude[:, :span] = near_amplitude[...]
    if density_in is not None:
        for start in range(tiles):
            tile_copy(start, True).wait()
    for start in range(tiles):
        columns = slice(start * step, (start + 1) * step)
        factor = stack([line for group in groups for line in lines(group, columns)])
        term = lax.dot_general(amplitude[...], factor, along, preferred_element_type=jnp.float32)
        term = term.reshape(local, rows, step)
        density[:, :, columns] = term if density_in is None else density[:, :, columns] + term
        tile_copy(start, False).start()
    for start in range(tiles):
        tile_copy(start, False).wait()


def block_step(number, energies, own, pieces, density, stage=None, near=()):
    parts = len(own)
    local, rows, aux = own[0].shape
    vmem = pl.BlockSpec(memory_space=pltpu.VMEM)
    hbm = pl.BlockSpec(memory_space=pltpu.HBM)
    groups = 1 if stage == 1 else parts
    own = own[:1] if stage == 2 else own
    operands = [*energies, *own, *pieces, *near]
    specs = [vmem] * len(operands)
    wide = local * rows
    span = local * sum(piece.shape[1] for piece in pieces) // groups if pieces else wide
    tiles = max(k for k in range(1, 4) if aux % (128 * k) == 0)
    steps = max(k for k in range(1, 3) if aux % (128 * k) == 0)
    lines = {None: 2 * parts - 1, 1: parts, 2: parts - 1}[stage]
    prior = density is not None
    layout = (number, parts, len(pieces) // groups, steps, tiles, prior, stage)
    scratch = [pltpu.VMEM((lines * wide, span), jnp.float32)]
    aliases = {}
    if stage == 1:
        out_shape = [
            jax.ShapeDtypeStruct((wide, span), jnp.bfloat16),
            jax.ShapeDtypeStruct(((parts - 1) * wide, span), jnp.bfloat16),
        ]
        out_specs = [vmem, vmem]
    else:
        out_shape = jax.ShapeDtypeStruct((local, rows, aux), jnp.float32)
        out_specs = hbm
        scratch += [
            pltpu.VMEM((wide, parts * span), jnp.bfloat16),
            pltpu.VMEM((local, rows, aux), jnp.float32),
            pltpu.SemaphoreType.DMA((tiles,)),
            pltpu.SemaphoreType.DMA((tiles,)),
        ]
        if prior:
            aliases = {len(operands): 0}
            operands.append(density)
            specs.append(hbm)
    products = lines + (0 if stage == 1 else parts)
    return pl.pallas_call(
        functools.partial(block_kernel, layout),
        out_shape=out_shape,
        in_specs=specs,
        out_specs=out_specs,
        scratch_shapes=scratch,
        input_output_aliases=aliases,
        compiler_params=pltpu.CompilerParams(vmem_limit_bytes=24 * 1024 * 1024),
        cost_estimate=pl.CostEstimate(
            flops=2 * products * wide * span * aux,
            bytes_accessed=2 * (parts * (span + wide) + 4 * wide) * aux,
            transcendentals=0,
        ),
    )(*operands)


def on_device(order, parts, factors, occ_energy, vir_energy):
    local, rows, _ = factors.shape
    count = len(order)
    halves = 2
    core = lax.axis_index("occ")
    place = lax.axis_index("vir")
    onward = [(order[k], order[(k + 1) % count]) for k in range(count)]
    backward = [(target, source) for source, target in onward]
    links = (onward, backward)
    near_core = [[((k + shift) % parts, k) for k in range(parts)] for shift in range(1, parts)]

    first = cut(factors, halves)
    half = rows // halves
    held = [{}, {}]
    own = [factors]
    own += [lax.ppermute(factors, "occ", pairs) for pairs in near_core]
    blocks, shifts, ranges = [], [], []
    for step in range(1, count - 1 + last_cuts):
        at = min(step, count - 1)
        some = half // last_cuts if at == count - 1 else half
        distance = (at + 1) // 2
        begins = [half * ((at - 1 + way) % 2) + some * (step - at) for way in range(2)]
        shifts.append([-distance, distance])
        ranges.append([np.arange(begin, begin + some) for begin in begins])
        for way in range(2):
            source = held[way][at - 2] if at > 2 else first[(at - 1 + way) % 2]
            if some < half:
                source = lax.slice_in_dim(source, some * (step - at), some * (step - at + 1), axis=1)
            held[way][step] = lax.ppermute(source, "vir", links[way])
        arrived = [held[way][step] for way in range(2)]
        block = list(arrived)
        for pairs in near_core:
            for way in range(2):
                block.append(lax.ppermute(arrived[way], "occ", pairs))
        blocks.append(block)

    spots = jnp.asarray([order.index(k) for k in range(count)], jnp.int32)
    away = np.zeros((len(blocks) + 1, rows), np.int32)
    inner = np.tile(np.arange(rows, dtype=np.int32), (len(blocks) + 1, 1))
    for number, (pair, spans) in enumerate(zip(shifts, ranges), 1):
        line = np.concatenate([np.full(len(span), shift) for shift, span in zip(pair, spans)])
        away[number, : len(line)] = line
        inner[number, : len(line)] = np.concatenate(spans)
    sources = jnp.asarray(order, jnp.int32)[(spots[place] + jnp.arange(-count, count, dtype=jnp.int32)) % count]
    energy_table = vir_energy.reshape(count, rows)[sources]
    vir_rows = energy_table[away + count, inner][:, None, :]
    own_vir = lax.dynamic_slice_in_dim(vir_energy, place * rows, rows)[:, None]
    mine_first = jnp.roll(occ_energy, -core * local)
    occ_pairs = (mine_first[:local, None] + mine_first[None, :]).reshape(-1, 1, 1)
    energies = (jnp.broadcast_to(occ_pairs, occ_pairs.shape[:2] + (rows,)), own_vir, vir_rows)

    density = block_step(0, energies, own, [], None)
    for number, block in enumerate(blocks, 1):
        if number < len(blocks):
            density = block_step(number, energies, own, block, density)
        else:
            near = block_step(number, energies, own, block[: len(links)], None, 1)
            density = block_step(number, energies, own, block, density, 2, near)
    return density


def solution(mesh):
    order = ring_order(mesh, "vir")
    parts = mesh.shape["occ"]

    def whole_step(factors, occ_energy, vir_energy):
        return on_device(order, parts, factors, occ_energy, vir_energy)

    return jax.shard_map(
        whole_step,
        mesh=mesh,
        in_specs=(P(("frag", "occ"), "vir", None), P("frag"), P("frag")),
        out_specs=P(("frag", "occ"), "vir", None),
        check_vma=False,
    )
```

time: 371 us -> 165 us (0.44)
  waiting for transfers between devices: 277 us -> 84 us
  matrix products: 48.3 us -> 0 us
  Pallas kernels: 0 us -> 44.6 us
  between operations: 13.4 us -> 0.43 us
  local copies, waits for them, and re-layouts: 10.5 us -> 18.2 us
    all_gather x2 -> x0, waiting for transfers between devices: 220 us -> none  [the longest x1 181 us: on_device(): gathered = lax.all_gather(factors, 'vir', axis=1, tiled=True)]
    ppermute x0 -> x29, waiting for transfers between devices: none -> 84 us  [the longest x14 83.9 us: on_device(): held[way][step] = lax.ppermute(source, 'vir', links[way])]
    all_to_all x4 -> x0, waiting for transfers between devices: 56.3 us -> none  [loop_step(): lax.all_to_all(direct, 'vir', split_axis=2, concat_axis=1, tiled=True)]
    dot_general x8 -> x0, matrix products: 48.3 us -> none  [the longest x4 28.2 us: loop_step(): jnp.einsum('iab,bp->iap', amplitude, partner, preferred_element_type=jnp....]
    pallas_call x0 -> x10, Pallas kernels: none -> 44.6 us  [the longest x9 44.5 us: block_step(): pl.pallas_call(functools.partial(block_kernel, layout), out_shape=out_sha...]
    all_to_all x4 -> x0, starting transfers between devices: 16.7 us -> none  [loop_step(): lax.all_to_all(direct, 'vir', split_axis=2, concat_axis=1, tiled=True)]
    ppermute x0 -> x29, starting transfers between devices: none -> 16.3 us  [the longest x14 14.9 us: on_device(): held[way][step] = lax.ppermute(source, 'vir', links[way])]
    gather x0 -> x3, local copies, waits for them, and re-layouts: none -> 8.8 us  [the longest x1 6.92 us: on_device(): vir_rows = energy_table[away + count, inner][:, None, :]]
  transfers between devices with their start and end apart: 6 -> 29, of which waited for: 6 -> 12; matrix products, arithmetic and copies ran while one was open for 1% -> 7% of each run, Pallas kernels for 0% -> 24%
where the time goes in v1:
time: 165 us
  waiting for transfers between devices  84 us (51%)
  Pallas kernels  44.6 us (27%)
  local copies, waits for them, and re-layouts  18.2 us (11%)
  starting transfers between devices  16.3 us (10%)
    ppermute x14, waiting for transfers between devices, on_device(): held[way][step] = lax.ppermute(source, 'vir', links[way])  83.9 us
    pallas_call x9, Pallas kernels, block_step(): pl.pallas_call(functools.partial(block_kernel, layout), out_shape=out_sha...  44.5 us
    ppermute x14, starting transfers between devices, on_device(): held[way][step] = lax.ppermute(source, 'vir', links[way])  14.9 us
    unnamed x34, local copies, waits for them, and re-layouts  7.74 us
    gather x1, local copies, waits for them, and re-layouts, on_device(): vir_rows = energy_table[away + count, inner][:, None, :]  6.92 us
  transfers between devices with their start and end apart: 29, of which 12 were waited for; matrix products, arithmetic and copies ran while one was open for 7% of the time, Pallas kernels for 24%

profile of v1, /device:TPU:0, one launch (start us, length us, event | category | flops | bytes accessed | tf_op | source)
XLA Modules:
  0.0 165.1 jit_solution(2194808948441800785)
XLA Ops:
  0.0 0.5 collective-permute-start.10
  0.5 1.4 copy-done.1
  1.9 0.1 cut.1
  2.0 2.6 %collective-permute-start = (bf16[2,64,3072]{2,1,0:T(8,128)(2,1)S(1)}, bf16[2,64,3072]{2,1,0:T(8,128)(2,1)S(1)}, u32[]{:S(2)}, u32[]{:S(2)}) collective-permute-start(bf16[2,64,3072]{2,1,0:T(8,128)(2,1)S(1)} %get-tuple-element.9), channel_id=1, source_target_pairs={{0,2},{2,4},{4,6},{6,7},{7,5},{5,3},{3,1},{1,0},{8,10},{10,12},{12... | collective-permute-start | bytes 2359304 | tf_op jit(solution)/shard_map/ppermute | solution.py:234
  4.7 0.0 collective-permute-start.4
  4.7 2.0 %collective-permute-start.11 = (bf16[2,64,3072]{2,1,0:T(8,128)(2,1)S(1)}, bf16[2,64,3072]{2,1,0:T(8,128)(2,1)S(1)}, u32[]{:S(2)}, u32[]{:S(2)}) collective-permute-start(bf16[2,64,3072]{2,1,0:T(8,128)(2,1)S(1)} %get-tuple-element.10), channel_id=1, source_target_pairs={{0,2},{2,4},{4,6},{6,7},{7,5},{5,3},{3,1},{1,0},{8,10},{10,12},{12... | collective-permute-start | bytes 2359304 | tf_op jit(solution)/shard_map/ppermute | solution.py:234
  6.7 0.0 collective-permute-start.14
  6.7 16.3 %collective-permute-done.refs_2_ = bf16[2,64,3072]{2,1,0:T(8,128)(2,1)S(1)} collective-permute-done((bf16[2,64,3072]{2,1,0:T(8,128)(2,1)S(1)}, bf16[2,64,3072]{2,1,0:T(8,128)(2,1)S(1)}, u32[]{:S(2)}, u32[]{:S(2)}) %collective-permute-start) | collective-permute-done | bytes 786464 | tf_op jit(solution)/shard_map/ppermute | solution.py:234
  23.0 2.1 %collective-permute-done.4.refs_3_ = bf16[2,64,3072]{2,1,0:T(8,128)(2,1)S(1)} collective-permute-done((bf16[2,64,3072]{2,1,0:T(8,128)(2,1)S(1)}, bf16[2,64,3072]{2,1,0:T(8,128)(2,1)S(1)}, u32[]{:S(2)}, u32[]{:S(2)}) %collective-permute-start.4) | collective-permute-done | bytes 786464 | tf_op jit(solution)/shard_map/ppermute | solution.py:234
  25.1 0.0 collective-permute-start.28
  25.1 14.6 %collective-permute-done.11.refs_2_ = bf16[2,64,3072]{2,1,0:T(8,128)(2,1)S(1)} collective-permute-done((bf16[2,64,3072]{2,1,0:T(8,128)(2,1)S(1)}, bf16[2,64,3072]{2,1,0:T(8,128)(2,1)S(1)}, u32[]{:S(2)}, u32[]{:S(2)}) %collective-permute-start.11) | collective-permute-done | bytes 786464 | tf_op jit(solution)/shard_map/ppermute | solution.py:234
  39.7 0.0 collective-permute-start.25
  39.7 1.6 collective-permute-done.14.refs_3_
  41.3 1.6 collective-permute-start.1
  42.9 0.9 copy-done.5
  43.7 0.4 collective-permute-start.5
  44.2 0.9 copy-done.7
  45.1 0.0 collective-permute-done.27.refs_4_
  45.1 0.9 copy-done.11
  46.0 1.6 collective-permute-start.12
  47.6 0.9 copy-done.3
  48.5 0.9 copy-done.13
  49.4 0.9 copy-done.9
  50.3 0.4 collective-permute-start.15
  50.7 11.1 %collective-permute-done.1.refs_2_ = bf16[2,64,3072]{2,1,0:T(8,128)(2,1)} collective-permute-done((bf16[2,64,3072]{2,1,0:T(8,128)(2,1)S(1)}, bf16[2,64,3072]{2,1,0:T(8,128)(2,1)}, u32[]{:S(2)}, u32[]{:S(2)}) %collective-permute-start.1) | collective-permute-done | bytes 786464 | tf_op jit(solution)/shard_map/ppermute | solution.py:234
  61.8 2.5 %collective-permute-done.5.refs_3_ = bf16[2,64,3072]{2,1,0:T(8,128)(2,1)} collective-permute-done((bf16[2,64,3072]{2,1,0:T(8,128)(2,1)S(1)}, bf16[2,64,3072]{2,1,0:T(8,128)(2,1)}, u32[]{:S(2)}, u32[]{:S(2)}) %collective-permute-start.5) | collective-permute-done | bytes 786464 | tf_op jit(solution)/shard_map/ppermute | solution.py:234
  64.3 12.8 %collective-permute-done.12.refs_2_ = bf16[2,64,3072]{2,1,0:T(8,128)(2,1)} collective-permute-done((bf16[2,64,3072]{2,1,0:T(8,128)(2,1)S(1)}, bf16[2,64,3072]{2,1,0:T(8,128)(2,1)}, u32[]{:S(2)}, u32[]{:S(2)}) %collective-permute-start.12) | collective-permute-done | bytes 786464 | tf_op jit(solution)/shard_map/ppermute | solution.py:234
  77.1 0.0 collective-permute-start.21
  77.1 0.9 copy-done.15
  78.0 1.6 collective-permute-start.2
  79.6 0.2 collective-permute-start.22
  79.8 0.4 collective-permute-start.6
  80.3 0.8 pad_add_fusion
  81.1 0.1 dynamic_slice.10
  81.1 1.2 dynamic_slice.12
  82.4 0.1 broadcast_add_fusion
  82.5 1.6 collective-permute-start.13
  84.0 0.7 fusion.1
  84.7 0.1 add.109
  84.8 1.3 gather_fusion
  86.1 0.5 collective-permute-start.16
  86.6 12.1 %collective-permute-done.2.refs_2_ = bf16[2,64,3072]{2,1,0:T(8,128)(2,1)} collective-permute-done((bf16[2,64,3072]{2,1,0:T(8,128)(2,1)}, bf16[2,64,3072]{2,1,0:T(8,128)(2,1)}, u32[]{:S(2)}, u32[]{:S(2)}) %collective-permute-start.2) | collective-permute-done | bytes 786464 | tf_op jit(solution)/shard_map/ppermute | solution.py:234
  98.7 1.6 collective-permute-start.3
  100.4 0.2 collective-permute-done.6.refs_3_
  100.5 0.4 collective-permute-start.7
  101.0 0.1 dynamic-slice_bitcast_fusion
  101.1 0.1 copy.34.own_vir
  101.2 0.6 gather_fusion.1
  101.8 6.9 %gather_fusion.2 = s32[1024]{0:T(1024)S(1)} fusion(s32[16,128]{1,0:T(8,128)S(1)} %gather_fusion.1, s32[1024]{0:T(1024)} %constant.98), kind=kCustom, calls=%fused_computation.2 | custom fusion | bytes 16384 | tf_op jit(solution)/shard_map/gather | solution.py:251
  108.7 0.1 broadcast_in_dim.10.occ_pairs
  108.8 4.0 %shard_map.92.refs_6_ = f32[2,128,3072]{2,1,0:T(8,128)} custom-call(s32[8,1,128]{2,1,0:T(1,128)S(1)} %broadcast_in_dim.10.occ_pairs, s32[128,1]{1,0:T(8,128)S(1)} %copy.34.own_vir, s32[8,1,128]{2,1,0:T(1,128)S(1)} %bitcast.13, bf16[2,128,3072]{2,1,0:T(8,128)(2,1)S(1)} %copy-done.2, bf16[2,128,3072]{2,1,0:T(8,128)(2,1)S(1)} %collective-permute-done.10.refs_1_), custom_call_target="tpu_custom_call" | custom-call | flops 2013265920 | bytes 12582912 | tf_op jit(solution)/shard_map/pallas_call | solution.py:190
  112.8 2.7 %collective-permute-done.13.refs_2_ = bf16[2,64,3072]{2,1,0:T(8,128)(2,1)} collective-permute-done((bf16[2,64,3072]{2,1,0:T(8,128)(2,1)}, bf16[2,64,3072]{2,1,0:T(8,128)(2,1)}, u32[]{:S(2)}, u32[]{:S(2)}) %collective-permute-start.13) | collective-permute-done | bytes 786464 | tf_op jit(solution)/shard_map/ppermute | solution.py:234
  115.6 4.1 %shard_map.93.refs_6_ = f32[2,128,3072]{2,1,0:T(8,128)} custom-call(s32[8,1,128]{2,1,0:T(1,128)S(1)} %broadcast_in_dim.10.occ_pairs, s32[128,1]{1,0:T(8,128)S(1)} %copy.34.own_vir, s32[8,1,128]{2,1,0:T(1,128)S(1)} %bitcast.14, bf16[2,128,3072]{2,1,0:T(8,128)(2,1)S(1)} %copy-done.2, ...), custom_call_target="tpu_custom_call", output_to_operand_aliasing={{}: (9, {})} | custom-call | flops 2013265920 | bytes 12582912 | tf_op jit(solution)/shard_map/pallas_call | solution.py:190
  119.7 0.6 collective-permute-start.17
  120.3 0.1 collective-permute-start.18
  120.4 5.2 %shard_map.94.refs_6_ = f32[2,128,3072]{2,1,0:T(8,128)} custom-call(s32[8,1,128]{2,1,0:T(1,128)S(1)} %broadcast_in_dim.10.occ_pairs, s32[128,1]{1,0:T(8,128)S(1)} %copy.34.own_vir, s32[8,1,128]{2,1,0:T(1,128)S(1)} %bitcast.15, bf16[2,128,3072]{2,1,0:T(8,128)(2,1)S(1)} %copy-done.2, ...), custom_call_target="tpu_custom_call", output_to_operand_aliasing={{}: (9, {})} | custom-call | flops 2013265920 | bytes 12582912 | tf_op jit(solution)/shard_map/pallas_call | solution.py:190
  125.6 6.4 %collective-permute-done.3.refs_2_.refs_1_ = bf16[2,64,3072]{2,1,0:T(8,128)(2,1)} collective-permute-done((bf16[2,64,3072]{2,1,0:T(8,128)(2,1)}, bf16[2,64,3072]{2,1,0:T(8,128)(2,1)}, u32[]{:S(2)}, u32[]{:S(2)}) %collective-permute-start.3) | collective-permute-done | bytes 786464 | tf_op jit(solution)/shard_map/ppermute | solution.py:234
  132.0 1.6 collective-permute-done.7.refs_3_.refs_2_
  133.6 5.9 %shard_map.95.refs_6_ = f32[2,128,3072]{2,1,0:T(8,128)} custom-call(s32[8,1,128]{2,1,0:T(1,128)S(1)} %broadcast_in_dim.10.occ_pairs, s32[128,1]{1,0:T(8,128)S(1)} %copy.34.own_vir, s32[8,1,128]{2,1,0:T(1,128)S(1)} %bitcast.16, bf16[2,128,3072]{2,1,0:T(8,128)(2,1)S(1)} %copy-done.2, ...), custom_call_target="tpu_custom_call", output_to_operand_aliasing={{}: (9, {})} | custom-call | flops 2013265920 | bytes 12582912 | tf_op jit(solution)/shard_map/pallas_call | solution.py:190
  139.5 5.9 %shard_map.96.refs_6_ = f32[2,128,3072]{2,1,0:T(8,128)} custom-call(s32[8,1,128]{2,1,0:T(1,128)S(1)} %broadcast_in_dim.10.occ_pairs, s32[128,1]{1,0:T(8,128)S(1)} %copy.34.own_vir, s32[8,1,128]{2,1,0:T(1,128)S(1)} %bitcast.17, bf16[2,128,3072]{2,1,0:T(8,128)(2,1)S(1)} %copy-done.2, ...), custom_call_target="tpu_custom_call", output_to_operand_aliasing={{}: (9, {})} | custom-call | flops 2013265920 | bytes 12582912 | tf_op jit(solution)/shard_map/pallas_call | solution.py:190
  145.4 2.7 %shard_map.91 = (bf16[256,256]{1,0:T(8,128)(2,1)S(1)}, bf16[256,256]{1,0:T(8,128)(2,1)S(1)}) custom-call(s32[8,1,128]{2,1,0:T(1,128)S(1)} %broadcast_in_dim.10.occ_pairs, s32[128,1]{1,0:T(8,128)S(1)} %copy.34.own_vir, s32[8,1,128]{2,1,0:T(1,128)S(1)} %bitcast.18, bf16[2,128,3072]{2,1,0:T(8,128)(2,1)S(1)} %copy-done.2, ...), custom_call_target="tpu_custom_call" | custom-call | flops 805306368 | bytes 12582912 | tf_op jit(solution)/shard_map/pallas_call | solution.py:190
  148.1 5.7 %shard_map.97.refs_6_ = f32[2,128,3072]{2,1,0:T(8,128)} custom-call(s32[8,1,128]{2,1,0:T(1,128)S(1)} %broadcast_in_dim.10.occ_pairs, s32[128,1]{1,0:T(8,128)S(1)} %copy.34.own_vir, s32[8,1,128]{2,1,0:T(1,128)S(1)} %bitcast.19, bf16[2,128,3072]{2,1,0:T(8,128)(2,1)S(1)} %copy-done.2, ...), custom_call_target="tpu_custom_call", output_to_operand_aliasing={{}: (9, {})} | custom-call | flops 2013265920 | bytes 12582912 | tf_op jit(solution)/shard_map/pallas_call | solution.py:190
  153.8 5.7 %shard_map.98.refs_7_ = f32[2,128,3072]{2,1,0:T(8,128)} custom-call(s32[8,1,128]{2,1,0:T(1,128)S(1)} %broadcast_in_dim.10.occ_pairs, s32[128,1]{1,0:T(8,128)S(1)} %copy.34.own_vir, s32[8,1,128]{2,1,0:T(1,128)S(1)} %bitcast.20, bf16[2,128,3072]{2,1,0:T(8,128)(2,1)S(1)} %copy-done.2, ...), custom_call_target="tpu_custom_call", output_to_operand_aliasing={{}: (9, {})} | custom-call | flops 2013265920 | bytes 12582912 | tf_op jit(solution)/shard_map/pallas_call | solution.py:190
  159.5 5.4 %shard_map.99 = f32[2,128,3072]{2,1,0:T(8,128)} custom-call(s32[8,1,128]{2,1,0:T(1,128)S(1)} %broadcast_in_dim.10.occ_pairs, s32[128,1]{1,0:T(8,128)S(1)} %copy.34.own_vir, s32[8,1,128]{2,1,0:T(1,128)S(1)} %bitcast.21, bf16[2,128,3072]{2,1,0:T(8,128)(2,1)S(1)} %copy-done.2, ...), custom_call_target="tpu_custom_call", output_to_operand_aliasing={{}: (10, {})} | custom-call | flops 1207959552 | bytes 12582912 | tf_op jit(solution)/shard_map/pallas_call | solution.py:190
  (53 shorter events, 0.1 us)
Async XLA Ops:
  0.0 101.0 %copy-start = (s32[1024]{0:T(1024)S(1)}, s32[1024]{0:T(1024)}, u32[]{:S(2)}) copy-start(s32[1024]{0:T(1024)} %param.11) | copy-start | bytes 12292
  0.0 43.7 %collective-permute-start.10 = (bf16[2,128,3072]{2,1,0:T(8,128)(2,1)}, bf16[2,128,3072]{2,1,0:T(8,128)(2,1)S(1)}, u32[]{:S(2)}, u32[]{:S(2)}) collective-permute-start(bf16[2,128,3072]{2,1,0:T(8,128)(2,1)} %refs_0_.17), channel_id=1, source_target_pairs={{8,0},{0,8},{9,1},{1,9},{10,2},{2,10},{11,3},{3,11},{12,4},{4,12},... | collective-permute-start | bytes 4718600 | tf_op jit(solution)/shard_map/ppermute | solution.py:221
  0.5 1.4 copy-start.1
  1.9 106.9 %copy-start.2 = (bf16[2,128,3072]{2,1,0:T(8,128)(2,1)S(1)}, bf16[2,128,3072]{2,1,0:T(8,128)(2,1)}, u32[]{:S(2)}) copy-start(bf16[2,128,3072]{2,1,0:T(8,128)(2,1)} %refs_0_.17) | copy-start | bytes 4718596
  2.0 21.0 %collective-permute-start = (bf16[2,64,3072]{2,1,0:T(8,128)(2,1)S(1)}, bf16[2,64,3072]{2,1,0:T(8,128)(2,1)S(1)}, u32[]{:S(2)}, u32[]{:S(2)}) collective-permute-start(bf16[2,64,3072]{2,1,0:T(8,128)(2,1)S(1)} %get-tuple-element.9), channel_id=1, source_target_pairs={{0,2},{2,4},{4,6},{6,7},{7,5},{5,3},{3,1},{1,0},{8,10},{10,12},{12... | collective-permute-start | bytes 2359304 | tf_op jit(solution)/shard_map/ppermute | solution.py:234
  4.7 20.4 %collective-permute-start.4 = (bf16[2,64,3072]{2,1,0:T(8,128)(2,1)S(1)}, bf16[2,64,3072]{2,1,0:T(8,128)(2,1)S(1)}, u32[]{:S(2)}, u32[]{:S(2)}) collective-permute-start(bf16[2,64,3072]{2,1,0:T(8,128)(2,1)S(1)} %get-tuple-element.10), channel_id=1, source_target_pairs={{2,0},{4,2},{6,4},{7,6},{5,7},{3,5},{1,3},{0,1},{10,8},{12,10},{14... | collective-permute-start | bytes 2359304 | tf_op jit(solution)/shard_map/ppermute | solution.py:234
  4.7 35.0 %collective-permute-start.11 = (bf16[2,64,3072]{2,1,0:T(8,128)(2,1)S(1)}, bf16[2,64,3072]{2,1,0:T(8,128)(2,1)S(1)}, u32[]{:S(2)}, u32[]{:S(2)}) collective-permute-start(bf16[2,64,3072]{2,1,0:T(8,128)(2,1)S(1)} %get-tuple-element.10), channel_id=1, source_target_pairs={{0,2},{2,4},{4,6},{6,7},{7,5},{5,3},{3,1},{1,0},{8,10},{10,12},{12... | collective-permute-start | bytes 2359304 | tf_op jit(solution)/shard_map/ppermute | solution.py:234
  6.7 34.6 %collective-permute-start.14 = (bf16[2,64,3072]{2,1,0:T(8,128)(2,1)S(1)}, bf16[2,64,3072]{2,1,0:T(8,128)(2,1)}, u32[]{:S(2)}, u32[]{:S(2)}) collective-permute-start(bf16[2,64,3072]{2,1,0:T(8,128)(2,1)S(1)} %get-tuple-element.9), channel_id=1, source_target_pairs={{2,0},{4,2},{6,4},{7,6},{5,7},{3,5},{1,3},{0,1},{10,8},{12,10},{14... | collective-permute-start | bytes 2359304 | tf_op jit(solution)/shard_map/ppermute | solution.py:234
  23.0 22.1 %collective-permute-start.27 = (bf16[2,64,3072]{2,1,0:T(8,128)(2,1)S(1)}, bf16[2,64,3072]{2,1,0:T(8,128)(2,1)S(1)}, u32[]{:S(2)}, u32[]{:S(2)}) collective-permute-start(bf16[2,64,3072]{2,1,0:T(8,128)(2,1)S(1)} %collective-permute-done.refs_2_), channel_id=1, source_target_pairs={{8,0},{0,8},{9,1},{1,9},{10,2},{2,10},{11,3},{3,11},{12,4},{4,12},... | collective-permute-start | bytes 2359304 | tf_op jit(solution)/shard_map/ppermute | solution.py:239
  25.1 23.4 %collective-permute-start.28 = (bf16[2,64,3072]{2,1,0:T(8,128)(2,1)S(1)}, bf16[2,64,3072]{2,1,0:T(8,128)(2,1)S(1)}, u32[]{:S(2)}, u32[]{:S(2)}) collective-permute-start(bf16[2,64,3072]{2,1,0:T(8,128)(2,1)S(1)} %collective-permute-done.4.refs_3_), channel_id=1, source_target_pairs={{8,0},{0,8},{9,1},{1,9},{10,2},{2,10},{11,3},{3,11},{12,4},{4,12},... | collective-permute-start | bytes 2359304 | tf_op jit(solution)/shard_map/ppermute | solution.py:239
  39.7 9.7 %collective-permute-start.25 = (bf16[2,64,3072]{2,1,0:T(8,128)(2,1)S(1)}, bf16[2,64,3072]{2,1,0:T(8,128)(2,1)S(1)}, u32[]{:S(2)}, u32[]{:S(2)}) collective-permute-start(bf16[2,64,3072]{2,1,0:T(8,128)(2,1)S(1)} %collective-permute-done.11.refs_2_), channel_id=1, source_target_pairs={{8,0},{0,8},{9,1},{1,9},{10,2},{2,10},{11,3},{3,11},{12,4},{4,12},... | collective-permute-start | bytes 2359304 | tf_op jit(solution)/shard_map/ppermute | solution.py:239
  41.3 20.5 %collective-permute-start.1 = (bf16[2,64,3072]{2,1,0:T(8,128)(2,1)S(1)}, bf16[2,64,3072]{2,1,0:T(8,128)(2,1)}, u32[]{:S(2)}, u32[]{:S(2)}) collective-permute-start(bf16[2,64,3072]{2,1,0:T(8,128)(2,1)S(1)} %collective-permute-done.refs_2_), channel_id=1, source_target_pairs={{0,2},{2,4},{4,6},{6,7},{7,5},{5,3},{3,1},{1,0},{8,10},{10,12},{12... | collective-permute-start | bytes 2359304 | tf_op jit(solution)/shard_map/ppermute | solution.py:234
  42.9 0.9 copy-start.5
  43.7 20.5 %collective-permute-start.5 = (bf16[2,64,3072]{2,1,0:T(8,128)(2,1)S(1)}, bf16[2,64,3072]{2,1,0:T(8,128)(2,1)}, u32[]{:S(2)}, u32[]{:S(2)}) collective-permute-start(bf16[2,64,3072]{2,1,0:T(8,128)(2,1)S(1)} %collective-permute-done.4.refs_3_), channel_id=1, source_target_pairs={{2,0},{4,2},{6,4},{7,6},{5,7},{3,5},{1,3},{0,1},{10,8},{12,10},{14... | collective-permute-start | bytes 2359304 | tf_op jit(solution)/shard_map/ppermute | solution.py:234
  44.2 0.9 copy-start.7
  45.1 0.9 copy-start.11
  46.0 31.0 %collective-permute-start.12 = (bf16[2,64,3072]{2,1,0:T(8,128)(2,1)S(1)}, bf16[2,64,3072]{2,1,0:T(8,128)(2,1)}, u32[]{:S(2)}, u32[]{:S(2)}) collective-permute-start(bf16[2,64,3072]{2,1,0:T(8,128)(2,1)S(1)} %collective-permute-done.11.refs_2_), channel_id=1, source_target_pairs={{0,2},{2,4},{4,6},{6,7},{7,5},{5,3},{3,1},{1,0},{8,10},{10,12},{12... | collective-permute-start | bytes 2359304 | tf_op jit(solution)/shard_map/ppermute | solution.py:234
  47.6 0.9 copy-start.3
  48.5 0.9 copy-start.13
  49.4 27.7 %collective-permute-start.26 = (bf16[2,64,3072]{2,1,0:T(8,128)(2,1)}, bf16[2,64,3072]{2,1,0:T(8,128)(2,1)S(1)}, u32[]{:S(2)}, u32[]{:S(2)}) collective-permute-start(bf16[2,64,3072]{2,1,0:T(8,128)(2,1)} %collective-permute-done.14.refs_3_), channel_id=1, source_target_pairs={{8,0},{0,8},{9,1},{1,9},{10,2},{2,10},{11,3},{3,11},{12,4},{4,12},... | collective-permute-start | bytes 2359304 | tf_op jit(solution)/shard_map/ppermute | solution.py:239
  49.4 0.9 copy-start.9
  50.3 29.3 %collective-permute-start.15 = (bf16[2,64,3072]{2,1,0:T(8,128)(2,1)}, bf16[2,64,3072]{2,1,0:T(8,128)(2,1)}, u32[]{:S(2)}, u32[]{:S(2)}) collective-permute-start(bf16[2,64,3072]{2,1,0:T(8,128)(2,1)} %collective-permute-done.14.refs_3_), channel_id=1, source_target_pairs={{2,0},{4,2},{6,4},{7,6},{5,7},{3,5},{1,3},{0,1},{10,8},{12,10},{14... | collective-permute-start | bytes 2359304 | tf_op jit(solution)/shard_map/ppermute | solution.py:234
  61.8 18.0 %collective-permute-start.23 = (bf16[2,64,3072]{2,1,0:T(8,128)(2,1)}, bf16[2,64,3072]{2,1,0:T(8,128)(2,1)}, u32[]{:S(2)}, u32[]{:S(2)}) collective-permute-start(bf16[2,64,3072]{2,1,0:T(8,128)(2,1)} %collective-permute-done.1.refs_2_), channel_id=1, source_target_pairs={{8,0},{0,8},{9,1},{1,9},{10,2},{2,10},{11,3},{3,11},{12,4},{4,12},... | collective-permute-start | bytes 2359304 | tf_op jit(solution)/shard_map/ppermute | solution.py:239
  64.3 18.2 %collective-permute-start.24 = (bf16[2,64,3072]{2,1,0:T(8,128)(2,1)}, bf16[2,64,3072]{2,1,0:T(8,128)(2,1)}, u32[]{:S(2)}, u32[]{:S(2)}) collective-permute-start(bf16[2,64,3072]{2,1,0:T(8,128)(2,1)} %collective-permute-done.5.refs_3_), channel_id=1, source_target_pairs={{8,0},{0,8},{9,1},{1,9},{10,2},{2,10},{11,3},{3,11},{12,4},{4,12},... | collective-permute-start | bytes 2359304 | tf_op jit(solution)/shard_map/ppermute | solution.py:239
  77.1 9.0 %collective-permute-start.21 = (bf16[2,64,3072]{2,1,0:T(8,128)(2,1)}, bf16[2,64,3072]{2,1,0:T(8,128)(2,1)}, u32[]{:S(2)}, u32[]{:S(2)}) collective-permute-start(bf16[2,64,3072]{2,1,0:T(8,128)(2,1)} %collective-permute-done.12.refs_2_), channel_id=1, source_target_pairs={{8,0},{0,8},{9,1},{1,9},{10,2},{2,10},{11,3},{3,11},{12,4},{4,12},... | collective-permute-start | bytes 2359304 | tf_op jit(solution)/shard_map/ppermute | solution.py:239
  77.1 0.9 copy-start.15
  78.0 20.7 %collective-permute-start.2 = (bf16[2,64,3072]{2,1,0:T(8,128)(2,1)}, bf16[2,64,3072]{2,1,0:T(8,128)(2,1)}, u32[]{:S(2)}, u32[]{:S(2)}) collective-permute-start(bf16[2,64,3072]{2,1,0:T(8,128)(2,1)} %collective-permute-done.1.refs_2_), channel_id=1, source_target_pairs={{0,2},{2,4},{4,6},{6,7},{7,5},{5,3},{3,1},{1,0},{8,10},{10,12},{12... | collective-permute-start | bytes 2359304 | tf_op jit(solution)/shard_map/ppermute | solution.py:234
  79.6 19.2 %collective-permute-start.22 = (bf16[2,64,3072]{2,1,0:T(8,128)(2,1)}, bf16[2,64,3072]{2,1,0:T(8,128)(2,1)}, u32[]{:S(2)}, u32[]{:S(2)}) collective-permute-start(bf16[2,64,3072]{2,1,0:T(8,128)(2,1)} %collective-permute-done.15.refs_3_), channel_id=1, source_target_pairs={{8,0},{0,8},{9,1},{1,9},{10,2},{2,10},{11,3},{3,11},{12,4},{4,12},... | collective-permute-start | bytes 2359304 | tf_op jit(solution)/shard_map/ppermute | solution.py:239
  79.8 20.7 %collective-permute-start.6 = (bf16[2,64,3072]{2,1,0:T(8,128)(2,1)}, bf16[2,64,3072]{2,1,0:T(8,128)(2,1)}, u32[]{:S(2)}, u32[]{:S(2)}) collective-permute-start(bf16[2,64,3072]{2,1,0:T(8,128)(2,1)} %collective-permute-done.5.refs_3_), channel_id=1, source_target_pairs={{2,0},{4,2},{6,4},{7,6},{5,7},{3,5},{1,3},{0,1},{10,8},{12,10},{14... | collective-permute-start | bytes 2359304 | tf_op jit(solution)/shard_map/ppermute | solution.py:234
  82.5 33.1 %collective-permute-start.13 = (bf16[2,64,3072]{2,1,0:T(8,128)(2,1)}, bf16[2,64,3072]{2,1,0:T(8,128)(2,1)}, u32[]{:S(2)}, u32[]{:S(2)}) collective-permute-start(bf16[2,64,3072]{2,1,0:T(8,128)(2,1)} %collective-permute-done.12.refs_2_), channel_id=1, source_target_pairs={{0,2},{2,4},{4,6},{6,7},{7,5},{5,3},{3,1},{1,0},{8,10},{10,12},{12... | collective-permute-start | bytes 2359304 | tf_op jit(solution)/shard_map/ppermute | solution.py:234
  86.1 33.6 %collective-permute-start.16 = (bf16[2,64,3072]{2,1,0:T(8,128)(2,1)}, bf16[2,64,3072]{2,1,0:T(8,128)(2,1)}, u32[]{:S(2)}, u32[]{:S(2)}) collective-permute-start(bf16[2,64,3072]{2,1,0:T(8,128)(2,1)} %collective-permute-done.15.refs_3_), channel_id=1, source_target_pairs={{2,0},{4,2},{6,4},{7,6},{5,7},{3,5},{1,3},{0,1},{10,8},{12,10},{14... | collective-permute-start | bytes 2359304 | tf_op jit(solution)/shard_map/ppermute | solution.py:234
  98.7 21.5 %collective-permute-start.19 = (bf16[2,64,3072]{2,1,0:T(8,128)(2,1)}, bf16[2,64,3072]{2,1,0:T(8,128)(2,1)}, u32[]{:S(2)}, u32[]{:S(2)}) collective-permute-start(bf16[2,64,3072]{2,1,0:T(8,128)(2,1)} %collective-permute-done.2.refs_2_), channel_id=1, source_target_pairs={{8,0},{0,8},{9,1},{1,9},{10,2},{2,10},{11,3},{3,11},{12,4},{4,12},... | collective-permute-start | bytes 2359304 | tf_op jit(solution)/shard_map/ppermute | solution.py:239
  98.7 33.2 %collective-permute-start.3 = (bf16[2,64,3072]{2,1,0:T(8,128)(2,1)}, bf16[2,64,3072]{2,1,0:T(8,128)(2,1)}, u32[]{:S(2)}, u32[]{:S(2)}) collective-permute-start(bf16[2,64,3072]{2,1,0:T(8,128)(2,1)} %collective-permute-done.2.refs_2_), channel_id=1, source_target_pairs={{0,2},{2,4},{4,6},{6,7},{7,5},{5,3},{3,1},{1,0},{8,10},{10,12},{12... | collective-permute-start | bytes 2359304 | tf_op jit(solution)/shard_map/ppermute | solution.py:234
  100.5 33.0 %collective-permute-start.7 = (bf16[2,64,3072]{2,1,0:T(8,128)(2,1)}, bf16[2,64,3072]{2,1,0:T(8,128)(2,1)}, u32[]{:S(2)}, u32[]{:S(2)}) collective-permute-start(bf16[2,64,3072]{2,1,0:T(8,128)(2,1)} %collective-permute-done.6.refs_3_), channel_id=1, source_target_pairs={{2,0},{4,2},{6,4},{7,6},{5,7},{3,5},{1,3},{0,1},{10,8},{12,10},{14... | collective-permute-start | bytes 2359304 | tf_op jit(solution)/shard_map/ppermute | solution.py:234
  108.8 6.8 %copy-start.6 = (bf16[2,64,3072]{2,1,0:T(8,128)(2,1)S(1)}, bf16[2,64,3072]{2,1,0:T(8,128)(2,1)}, u32[]{:S(2)}) copy-start(bf16[2,64,3072]{2,1,0:T(8,128)(2,1)} %copy-done.5) | copy-start | bytes 2359300
  108.8 6.8 %copy-start.8 = (bf16[2,64,3072]{2,1,0:T(8,128)(2,1)S(1)}, bf16[2,64,3072]{2,1,0:T(8,128)(2,1)}, u32[]{:S(2)}) copy-start(bf16[2,64,3072]{2,1,0:T(8,128)(2,1)} %copy-done.7) | copy-start | bytes 2359300
  108.8 6.8 %copy-start.12 = (bf16[2,64,3072]{2,1,0:T(8,128)(2,1)S(1)}, bf16[2,64,3072]{2,1,0:T(8,128)(2,1)}, u32[]{:S(2)}) copy-start(bf16[2,64,3072]{2,1,0:T(8,128)(2,1)} %copy-done.11) | copy-start | bytes 2359300
  108.8 6.8 %copy-start.14 = (bf16[2,64,3072]{2,1,0:T(8,128)(2,1)S(1)}, bf16[2,64,3072]{2,1,0:T(8,128)(2,1)}, u32[]{:S(2)}) copy-start(bf16[2,64,3072]{2,1,0:T(8,128)(2,1)} %copy-done.13) | copy-start | bytes 2359300
  112.8 7.5 %copy-start.4 = (bf16[2,64,3072]{2,1,0:T(8,128)(2,1)S(1)}, bf16[2,64,3072]{2,1,0:T(8,128)(2,1)}, u32[]{:S(2)}) copy-start(bf16[2,64,3072]{2,1,0:T(8,128)(2,1)} %copy-done.3) | copy-start | bytes 2359300
  112.8 7.5 %copy-start.10 = (bf16[2,64,3072]{2,1,0:T(8,128)(2,1)S(1)}, bf16[2,64,3072]{2,1,0:T(8,128)(2,1)}, u32[]{:S(2)}) copy-start(bf16[2,64,3072]{2,1,0:T(8,128)(2,1)} %copy-done.9) | copy-start | bytes 2359300
  112.8 7.5 %copy-start.16 = (bf16[2,64,3072]{2,1,0:T(8,128)(2,1)S(1)}, bf16[2,64,3072]{2,1,0:T(8,128)(2,1)}, u32[]{:S(2)}) copy-start(bf16[2,64,3072]{2,1,0:T(8,128)(2,1)} %copy-done.15) | copy-start | bytes 2359300
  115.6 32.5 %collective-permute-start.20 = (bf16[2,64,3072]{2,1,0:T(8,128)(2,1)}, bf16[2,64,3072]{2,1,0:T(8,128)(2,1)S(1)}, u32[]{:S(2)}, u32[]{:S(2)}) collective-permute-start(bf16[2,64,3072]{2,1,0:T(8,128)(2,1)} %collective-permute-done.6.refs_3_), channel_id=1, source_target_pairs={{8,0},{0,8},{9,1},{1,9},{10,2},{2,10},{11,3},{3,11},{12,4},{4,12},... | collective-permute-start | bytes 2359304 | tf_op jit(solution)/shard_map/ppermute | solution.py:239
  119.7 34.1 %collective-permute-start.17 = (bf16[2,64,3072]{2,1,0:T(8,128)(2,1)}, bf16[2,64,3072]{2,1,0:T(8,128)(2,1)S(1)}, u32[]{:S(2)}, u32[]{:S(2)}) collective-permute-start(bf16[2,64,3072]{2,1,0:T(8,128)(2,1)} %collective-permute-done.13.refs_2_), channel_id=1, source_target_pairs={{8,0},{0,8},{9,1},{1,9},{10,2},{2,10},{11,3},{3,11},{12,4},{4,12},... | collective-permute-start | bytes 2359304 | tf_op jit(solution)/shard_map/ppermute | solution.py:239
  120.3 33.5 %collective-permute-start.18 = (bf16[2,64,3072]{2,1,0:T(8,128)(2,1)}, bf16[2,64,3072]{2,1,0:T(8,128)(2,1)S(1)}, u32[]{:S(2)}, u32[]{:S(2)}) collective-permute-start(bf16[2,64,3072]{2,1,0:T(8,128)(2,1)} %collective-permute-done.16.refs_3_), channel_id=1, source_target_pairs={{8,0},{0,8},{9,1},{1,9},{10,2},{2,10},{11,3},{3,11},{12,4},{4,12},... | collective-permute-start | bytes 2359304 | tf_op jit(solution)/shard_map/ppermute | solution.py:239
  132.0 27.5 %collective-permute-start.8 = (bf16[2,64,3072]{2,1,0:T(8,128)(2,1)}, bf16[2,64,3072]{2,1,0:T(8,128)(2,1)S(1)}, u32[]{:S(2)}, u32[]{:S(2)}) collective-permute-start(bf16[2,64,3072]{2,1,0:T(8,128)(2,1)} %collective-permute-done.3.refs_2_.refs_1_), channel_id=1, source_target_pairs={{8,0},{0,8},{9,1},{1,9},{10,2},{2,10},{11,3},{3,11},{12,4},{4,12},... | collective-permute-start | bytes 2359304 | tf_op jit(solution)/shard_map/ppermute | solution.py:239
  133.6 25.9 %collective-permute-start.9 = (bf16[2,64,3072]{2,1,0:T(8,128)(2,1)}, bf16[2,64,3072]{2,1,0:T(8,128)(2,1)S(1)}, u32[]{:S(2)}, u32[]{:S(2)}) collective-permute-start(bf16[2,64,3072]{2,1,0:T(8,128)(2,1)} %collective-permute-done.7.refs_3_.refs_2_), channel_id=1, source_target_pairs={{8,0},{0,8},{9,1},{1,9},{10,2},{2,10},{11,3},{3,11},{12,4},{4,12},... | collective-permute-start | bytes 2359304 | tf_op jit(solution)/shard_map/ppermute | solution.py:239
